TPU v7x, 32 devices: a whole 2x2x4 slice. The times are simulated.
32 devices in a mesh: hi: 4 (over z), lo: 8 (over y, x, core).
Axes of the slice: x: 2, y: 2, z: 4, core: 2. Of those that a mesh axis runs over, the one named last changes fastest.
Arguments:
- state: float32 [2, 33554432], P(None, ('hi', 'lo')), may hold values from -6 to 6
Outputs:
- transformed: float32 [2, 33554432], P(None, ('hi', 'lo'))
All inputs are finite; a program needn't handle non-finite values.
Results may differ from a plain program's by a relative error of at most 0.0003.
Values sent between devices are 32-bit elements.
A program may use at most 128 MiB of HBM per device.

v0:
```python
import math

import jax
import jax.numpy as jnp
from jax import lax
from jax.sharding import PartitionSpec as P

SUB_A = 1024


def product(left, right):
    return jnp.dot(left, right, precision=lax.Precision.HIGHEST, preferred_element_type=jnp.float32)


def dft_table(length, factor):
    steps = jnp.arange(length, dtype=jnp.int32)
    indices = steps[:, None] * steps[None, :] % length
    phases = indices.astype(jnp.float32) * (2.0 * math.pi / length)
    return (jnp.cos(phases) * factor, jnp.sin(phases) * factor)


def rotate(real_part, imag_part, phases):
    cosine = jnp.cos(phases)
    sine = jnp.sin(phases)
    return (real_part * cosine - imag_part * sine, real_part * sine + imag_part * cosine)


def remap_entry(blocks):
    return lax.all_to_all(blocks, ("hi", "lo"), split_axis=1, concat_axis=1, tiled=True)


def remap_middle(blocks):
    return lax.all_to_all(blocks, ("hi", "lo"), split_axis=1, concat_axis=1, tiled=True)


def remap_final(blocks):
    return lax.all_to_all(blocks, ("hi", "lo"), split_axis=1, concat_axis=1, tiled=True)


def shards(state):
    count_high = lax.axis_size("hi")
    count_low = lax.axis_size("lo")
    devices_all = count_high * count_low
    device_pos = lax.axis_index("hi") * count_low + lax.axis_index("lo")
    amplitudes = state.shape[1]
    per_peer = amplitudes // devices_all
    whole_size = amplitudes * devices_all
    blocks = remap_entry(state.reshape(2, devices_all, per_peer))
    table_re, table_im = dft_table(devices_all, 1.0 / math.sqrt(devices_all))
    mixed_re = product(table_re, blocks[0]) - product(table_im, blocks[1])
    mixed_im = product(table_re, blocks[1]) + product(table_im, blocks[0])
    row_ids = jnp.arange(devices_all, dtype=jnp.int32)
    col_ids = device_pos * per_peer + jnp.arange(per_peer, dtype=jnp.int32)
    phases = (row_ids[:, None] * col_ids[None, :] % whole_size).astype(jnp.float32) * (
        2.0 * math.pi / whole_size
    )
    mixed_re, mixed_im = rotate(mixed_re, mixed_im, phases)
    gathered = remap_middle(jnp.stack([mixed_re, mixed_im]))
    outer_len = SUB_A
    inner_len = amplitudes // outer_len
    local_grid = gathered.reshape(2, outer_len, inner_len)
    outer_re, outer_im = dft_table(outer_len, 1.0 / math.sqrt(outer_len))
    half_re = product(outer_re, local_grid[0]) - product(outer_im, local_grid[1])
    half_im = product(outer_re, local_grid[1]) + product(outer_im, local_grid[0])
    outer_ids = jnp.arange(outer_len, dtype=jnp.int32)
    inner_ids = jnp.arange(inner_len, dtype=jnp.int32)
    phases = (outer_ids[:, None] * inner_ids[None, :] % amplitudes).astype(jnp.float32) * (
        2.0 * math.pi / amplitudes
    )
    half_re, half_im = rotate(half_re, half_im, phases)
    inner_re, inner_im = dft_table(inner_len, 1.0 / math.sqrt(inner_len))
    done_re = product(half_re, inner_re) - product(half_im, inner_im)
    done_im = product(half_re, inner_im) + product(half_im, inner_re)
    ordered = jnp.stack([done_re, done_im]).transpose(0, 2, 1).reshape(2, devices_all, per_peer)
    arrived = remap_final(ordered)
    return arrived.transpose(0, 2, 1).reshape(2, amplitudes)


def solution(mesh):
    placed = (P(None, ("hi", "lo")),)
    return jax.shard_map(
        shards, mesh=mesh, in_specs=placed, out_specs=P(None, ("hi", "lo")), check_vma=False
    )
```

profile of v0, /device:TPU:24, one launch (start us, length us, event | category | flops | bytes accessed | tf_op | source)
XLA Modules:
  0.0 1075.5 jit_solution(11624295385155374427)
XLA Ops:
  0.0 5.9 all-to-all-start
  6.0 181.4 %all-to-all-done = f32[2,32,32768]{2,0,1:T(2,128)} async-done(((f32[2,32,32768]{2,0,1:T(2,128)}), f32[2,32,32768]{2,0,1:T(2,128)}, u32[]{:S(2)}, u32[]{:S(2)}) %all-to-all-start) | async-done | bytes 8388640 | tf_op jit(solution)/shard_map/all_to_all | solution.py:29
  187.3 9.9 fusion.143
  197.2 5.9 fusion.11
  203.1 5.9 fusion.7
  209.0 6.1 convolution_add_fusion
  215.1 22.9 %subtract_bitcast_fusion.1 = (f32[1,32,32768]{2,1,0:T(8,128)S(1)}, f32[1,32,32768]{2,1,0:T(8,128)S(1)}) fusion(f32[32,32768]{1,0:T(8,128)S(1)} %convolution_add_fusion, s32[32768]{0:T(1024)S(1)} %iota_add_fusion, f32[32,32768]{1,0:T(8,128)S(1)} %fusion.11, f32[1,32,32768]{2,0,1:T(1,128)S(1)} %get-tuple-element.10), kind=kOutput, calls=%fused_computation.33 | convolution fusion | flops 424688640 | bytes 21102592 | tf_op jit(solution)/shard_map/dot_general | solution.py:12
  238.0 0.5 pad_maximum_fusion
  238.6 14.3 %copy.4 = f32[2,32,32768]{2,0,1:T(2,128)S(1)} copy(f32[2,32,32768]{2,1,0:T(8,128)S(1)} %pad_maximum_fusion) | data formatting | bytes 16777216 | tf_op jit(solution)/shard_map/stack | solution.py:58
  252.9 191.4 %all_to_all.15 = f32[2,32,32768]{2,0,1:T(2,128)} all-to-all(f32[2,32,32768]{2,0,1:T(2,128)S(1)} %copy.4), channel_id=1, replica_groups=mesh['hi'=4,'lo'=8] {'hi','lo'}, dimensions={1} | all-to-all | bytes 16777216 | tf_op jit(solution)/shard_map/all_to_all | solution.py:33
  444.3 28.8 %slice_reduce_fusion.1 = (f32[32,32768]{1,0:T(8,128)}, f32[32,32768]{1,0:T(8,128)}) fusion(f32[2,32,32768]{2,0,1:T(2,128)} %all_to_all.15), kind=kLoop, calls=%fused_computation.20 | loop fusion | bytes 16777216 | tf_op jit(solution)/shard_map/slice | solution.py:63
  473.1 4.9 squeeze.18
  478.0 4.9 squeeze.19
  483.0 31.5 %fusion.29 = f32[1024,1024]{1,0:T(8,128)S(1)} fusion(f32[1024,1024]{1,0:T(8,128)} %squeeze.19), kind=kOutput, calls=%fused_computation.52 | convolution fusion | flops 12900630528 | bytes 8388608 | tf_op jit(solution)/shard_map/dot_general | solution.py:12
  514.5 29.6 %fusion.30 = f32[1024,1024]{1,0:T(8,128)S(1)} fusion(f32[1024,1024]{1,0:T(8,128)S(1)} %copy-done), kind=kOutput, calls=%fused_computation.53 | convolution fusion | flops 12900630528 | bytes 8388608 | tf_op jit(solution)/shard_map/dot_general | solution.py:12
  544.2 29.2 %fusion.56 = f32[1024,1024]{1,0:T(8,128)S(1)} fusion(f32[1024,1024]{1,0:T(8,128)S(1)} %fusion.29, f32[1024,1024]{1,0:T(8,128)S(1)} %copy-done), kind=kOutput, calls=%fused_computation.71 | convolution fusion | flops 12901679104 | bytes 12582912 | tf_op jit(solution)/shard_map/dot_general | solution.py:12
  573.4 29.7 %fusion.55 = f32[1024,1024]{1,0:T(8,128)S(1)} fusion(f32[1024,1024]{1,0:T(8,128)S(1)} %fusion.30, f32[1024,1024]{1,0:T(8,128)S(1)} %copy-done.1), kind=kOutput, calls=%fused_computation.70 | convolution fusion | flops 12901679104 | bytes 12582912 | tf_op jit(solution)/shard_map/dot_general | solution.py:12
  603.1 16.8 %multiply_add_fusion.10 = f32[1024,1024]{1,0:T(8,128)S(1)} fusion(f32[1024,1024]{1,0:T(8,128)S(1)} %fusion.56, f32[1024,1024]{1,0:T(8,128)S(1)} %fusion.55), kind=kLoop, calls=%fused_computation.29.clone.clone.2 | loop fusion | flops 17825792 | bytes 12582912 | tf_op jit(solution)/shard_map/dot_general | solution.py:12
  619.9 16.8 %multiply_subtract_fusion.9 = f32[1024,1024]{1,0:T(8,128)S(1)} fusion(f32[1024,1024]{1,0:T(8,128)S(1)} %fusion.56, f32[1024,1024]{1,0:T(8,128)S(1)} %fusion.55), kind=kLoop, calls=%fused_computation.30.clone.clone.2 | loop fusion | flops 17825792 | bytes 12582912 | tf_op jit(solution)/shard_map/dot_general | solution.py:12
  636.8 16.8 %multiply_add_fusion.9 = f32[1024,1024]{1,0:T(8,128)S(1)} fusion(f32[1024,1024]{1,0:T(8,128)S(1)} %fusion.56, f32[1024,1024]{1,0:T(8,128)S(1)} %fusion.55), kind=kLoop, calls=%fused_computation.29.clone.1.clone.2 | loop fusion | flops 17825792 | bytes 12582912 | tf_op jit(solution)/shard_map/dot_general | solution.py:12
  653.6 16.8 %multiply_subtract_fusion.10 = f32[1024,1024]{1,0:T(8,128)S(1)} fusion(f32[1024,1024]{1,0:T(8,128)S(1)} %fusion.56, f32[1024,1024]{1,0:T(8,128)S(1)} %fusion.55), kind=kLoop, calls=%fused_computation.30.clone.1.clone.2 | loop fusion | flops 17825792 | bytes 12582912 | tf_op jit(solution)/shard_map/dot_general | solution.py:12
  670.4 31.3 %fusion.27 = f32[1024,1024]{1,0:T(8,128)S(1)} fusion(f32[1024,1024]{1,0:T(8,128)S(1)} %multiply_add_fusion.10), kind=kOutput, calls=%fused_computation.50 | convolution fusion | flops 12900630528 | bytes 8388608 | tf_op jit(solution)/shard_map/dot_general | solution.py:12
  701.8 31.4 %fusion.28 = f32[1024,1024]{1,0:T(8,128)S(1)} fusion(f32[1024,1024]{1,0:T(8,128)S(1)} %multiply_subtract_fusion.10), kind=kOutput, calls=%fused_computation.51 | convolution fusion | flops 12900630528 | bytes 8388608 | tf_op jit(solution)/shard_map/dot_general | solution.py:12
  733.2 31.5 %add_bitcast_fusion = f32[1,1024,1024]{2,1,0:T(8,128)S(1)} fusion(f32[1024,1024]{1,0:T(8,128)S(1)} %fusion.27, f32[1024,1024]{1,0:T(8,128)S(1)} %multiply_subtract_fusion.9), kind=kOutput, calls=%fused_computation.27 | convolution fusion | flops 12901679104 | bytes 12582912 | tf_op jit(solution)/shard_map/dot_general | solution.py:12
  764.7 31.3 %subtract_bitcast_fusion = f32[1,1024,1024]{2,1,0:T(8,128)S(1)} fusion(f32[1024,1024]{1,0:T(8,128)S(1)} %fusion.28, f32[1024,1024]{1,0:T(8,128)S(1)} %multiply_add_fusion.9), kind=kOutput, calls=%fused_computation.28 | convolution fusion | flops 12901679104 | bytes 12582912 | tf_op jit(solution)/shard_map/dot_general | solution.py:12
  796.0 4.2 maximum_bitcast_fusion
  800.2 8.7 copy.5
  808.9 9.4 reshape.19
  818.2 14.4 %copy.6 = f32[2,32,32768]{2,0,1:T(2,128)S(1)} copy(f32[2,32,32768]{2,1,0:T(8,128)} %reshape.19) | data formatting | bytes 16777216 | tf_op jit(solution)/shard_map/reshape | solution.py:74
  832.6 192.3 %all_to_all.16 = f32[2,32,32768]{2,0,1:T(2,128)} all-to-all(f32[2,32,32768]{2,0,1:T(2,128)S(1)} %copy.6), channel_id=1, replica_groups=mesh['hi'=4,'lo'=8] {'hi','lo'}, dimensions={1} | all-to-all | bytes 16777216 | tf_op jit(solution)/shard_map/all_to_all | solution.py:37
  1024.9 22.5 %copy.7 = f32[2,32768,32]{2,1,0:T(8,128)} copy(f32[2,32768,32]{1,0,2:T(2,128)} %bitcast.36) | data formatting | bytes 16777216 | tf_op jit(solution)/shard_map/transpose | solution.py:76
  1047.4 27.8 %reshape.20 = f32[2,1048576]{1,0:T(2,128)} reshape(f32[2,32768,32]{2,1,0:T(8,128)} %copy.7) | data formatting | bytes 16777216 | tf_op jit(solution)/shard_map/reshape | solution.py:76
  (5 shorter events, 0.0 us)
Async XLA Ops:
  0.0 187.3 %all-to-all-start = ((f32[2,32,32768]{2,0,1:T(2,128)}), f32[2,32,32768]{2,0,1:T(2,128)}, u32[]{:S(2)}, u32[]{:S(2)}) async-start(f32[2,32,32768]{2,0,1:T(2,128)} %bitcast.37), calls=%async_computation | async-start | bytes 16777216 | tf_op jit(solution)/shard_map/all_to_all | solution.py:29
  483.0 31.6 %copy-start = (f32[1024,1024]{1,0:T(8,128)S(1)}, f32[1024,1024]{1,0:T(8,128)}, u32[]{:S(2)}) copy-start(f32[1024,1024]{1,0:T(8,128)} %squeeze.18) | copy-start | bytes 12582916
  544.2 29.2 %copy-start.1 = (f32[1024,1024]{1,0:T(8,128)S(1)}, f32[1024,1024]{1,0:T(8,128)}, u32[]{:S(2)}) copy-start(f32[1024,1024]{1,0:T(8,128)} %squeeze.19) | copy-start | bytes 12582916
where the time goes:
time: 1090 us; the launch traced here: 1080 us
  blocking collectives  384 us (35%)
  matrix products  286 us (26%)
  waiting for transfers between devices  181 us (17%)
  local copies, waits for them, and re-layouts  146 us (13%)
  other arithmetic  72.1 us (7%)
    dot_general x12, matrix products, product(): jnp.dot(left, right, precision=lax.Precision.HIGHEST, preferred_element_t...  286 us
    all_to_all x1, blocking collectives, remap_final(): lax.all_to_all(blocks, ('hi', 'lo'), split_axis=1, concat_axis=1, tiled=T...  192 us
    all_to_all x1, blocking collectives, remap_middle(): lax.all_to_all(blocks, ('hi', 'lo'), split_axis=1, concat_axis=1, tiled=T...  191 us
    all_to_all x1, waiting for transfers between devices, remap_entry(): lax.all_to_all(blocks, ('hi', 'lo'), split_axis=1, concat_axis=1, tiled=T...  181 us
    dot_general x4, other arithmetic, product(): jnp.dot(left, right, precision=lax.Precision.HIGHEST, preferred_element_t...  67.3 us
    slice x1, local copies, waits for them, and re-layouts, shards(): local_grid[0]  28.8 us
    reshape x1, local copies, waits for them, and re-layouts, shards(): return arrived.transpose(0, 2, 1).reshape(2, amplitudes)  27.8 us
    reshape x2, local copies, waits for them, and re-layouts, shards(): jnp.stack([done_re, done_im]).transpose(0, 2, 1)  23.7 us
  transfers between devices with their start and end apart: 1, of which 1 were waited for; matrix products, arithmetic and copies ran while one was open for 0% of the time, Pallas kernels for 0%

commit v1 on v0

v1 whole, which is shorter than its diff:
```python
import math

import jax
import jax.numpy as jnp
import numpy as np
from jax import lax
from jax.sharding import PartitionSpec as P

LANES = 128


def product(spec, left, right):
    return jnp.einsum(spec, left, right, precision=lax.Precision.HIGH, preferred_element_type=jnp.float32)


def dft_table(length):
    steps = np.arange(length, dtype=np.int64)
    phases = (steps[:, None] * steps[None, :] % length) * (2.0 * math.pi / length)
    cosine, sine = np.cos(phases) / math.sqrt(length), np.sin(phases) / math.sqrt(length)
    table = np.stack([np.stack([cosine, -sine], 1), np.stack([sine, cosine], 1)])
    return table.astype(np.float32)


def unit(indices, length):
    phases = (indices % length).astype(jnp.float32) * (2.0 * math.pi / length)
    return jnp.cos(phases), jnp.sin(phases)


def fixed_unit(left, right, length):
    phases = (np.arange(left)[:, None] * np.arange(right)[None, :] % length) * (2.0 * math.pi / length)
    return np.cos(phases).astype(np.float32), np.sin(phases).astype(np.float32)


def times(left, right):
    return (left[0] * right[0] - left[1] * right[1], left[0] * right[1] + left[1] * right[0])


def swap(blocks):
    return lax.all_to_all(blocks, ("hi", "lo"), split_axis=1, concat_axis=1, tiled=True)


def shards(state):
    count_low = lax.axis_size("lo")
    count = lax.axis_size("hi") * count_low
    me = lax.axis_index("hi") * count_low + lax.axis_index("lo")
    amplitudes = state.shape[1]
    whole = amplitudes * count
    mid = amplitudes // (count * LANES)
    low = count * mid
    blocks = state.reshape(2, mid, count, LANES).transpose(0, 2, 1, 3)
    x = swap(blocks)
    x = product("vkut,utab->vkab", dft_table(count), x)
    rest = me * LANES + jnp.arange(LANES, dtype=jnp.int32)
    rest_re, rest_im = unit(jnp.arange(count, dtype=jnp.int32)[:, None] * rest[None, :], whole)
    own_re, own_im = fixed_unit(count, mid, low)
    turn = times((own_re[:, :, None], own_im[:, :, None]), (rest_re[:, None, :], rest_im[:, None, :]))
    x = jnp.stack(times((x[0], x[1]), turn))
    x = product("vkua,uqab->vkqb", dft_table(mid), x)
    turn = unit(jnp.arange(mid, dtype=jnp.int32)[:, None] * rest[None, :], whole // count)
    x = jnp.stack(times((x[0], x[1]), (turn[0][:, None, :], turn[1][:, None, :])))
    x = swap(x.reshape(2, count, mid, LANES))
    x = product("vkud,udqb->vkqb", dft_table(count), x)
    turn = fixed_unit(count, LANES, count * LANES)
    x = jnp.stack(times((x[0], x[1]), (turn[0][:, None, :], turn[1][:, None, :])))
    x = product("vkub,upqb->vkpq", dft_table(LANES), x)
    x = swap(x.reshape(2, count, LANES // count * count, mid))
    return x.transpose(0, 2, 1, 3).reshape(2, amplitudes)


def solution(mesh):
    placed = (P(None, ("hi", "lo")),)
    return jax.shard_map(
        shards, mesh=mesh, in_specs=placed, out_specs=P(None, ("hi", "lo")), check_vma=False
    )
```

time: 1090 us -> 717 us (0.66)
  matrix products: 286 us -> 40.2 us
  other arithmetic: 72.1 us -> 10.2 us
  local copies, waits for them, and re-layouts: 146 us -> 84.4 us
    dot_general x12 -> x4, matrix products: 286 us -> 40.2 us  [product(): jnp.einsum(spec, left, right, precision=lax.Precision.HIGH, preferred_ele...]
    dot_general x4 -> x0, other arithmetic: 67.3 us -> none  [product(): jnp.dot(left, right, precision=lax.Precision.HIGHEST, preferred_element_t...]
    reshape x3 -> x1, local copies, waits for them, and re-layouts: 51.6 us -> 0.98 us  [shards(): x = swap(x.reshape(2, count, LANES // count * count, mid))]
    slice x2 -> x0, local copies, waits for them, and re-layouts: 38.7 us -> none  [the longest x1 28.8 us: shards(): local_grid[0]]
    unnamed x4 -> x16, local copies, waits for them, and re-layouts: 0.01 us -> 27.6 us
    another operation x1, local copies, waits for them, and re-layouts: 14.3 us -> 31.5 us  [shards(): jnp.stack(times((x[0], x[1]), (turn[0][:, None, :], turn[1][:, None, :])))]
    transpose x2, local copies, waits for them, and re-layouts: 31.2 us -> 14.6 us  [the longest x1 9.75 us: shards(): blocks = state.reshape(2, mid, count, LANES).transpose(0, 2, 1, 3)]
where the time goes in v1:
time: 717 us; the launch traced here: 711 us
  blocking collectives  389 us (54%)
  waiting for transfers between devices  181 us (25%)
  local copies, waits for them, and re-layouts  84.4 us (12%)
  matrix products  40.2 us (6%)
  other arithmetic  10.2 us (1%)
    all_to_all x2, blocking collectives, swap(): lax.all_to_all(blocks, ('hi', 'lo'), split_axis=1, concat_axis=1, tiled=T...  389 us
    all_to_all x1, waiting for transfers between devices, swap(): lax.all_to_all(blocks, ('hi', 'lo'), split_axis=1, concat_axis=1, tiled=T...  181 us
    dot_general x4, matrix products, product(): jnp.einsum(spec, left, right, precision=lax.Precision.HIGH, preferred_ele...  40.2 us
    another operation x1, local copies, waits for them, and re-layouts, shards(): jnp.stack(times((x[0], x[1]), (turn[0][:, None, :], turn[1][:, None, :])))  31.5 us
    unnamed x16, local copies, waits for them, and re-layouts  27.6 us
  transfers between devices with their start and end apart: 1, of which 1 were waited for; matrix products, arithmetic and copies ran while one was open for 0% of the time, Pallas kernels for 0%

profile of v1, /device:TPU:24, one launch (start us, length us, event | category | flops | bytes accessed | tf_op | source)
XLA Modules:
  0.0 710.6 jit_solution(17996858690700084094)
XLA Ops:
  0.0 3.9 copy.47
  3.9 9.7 %copy.29 = f32[2,32,256,128]{3,0,2,1:T(2,128)} copy(f32[2,32,256,128]{3,1,2,0:T(8,128)S(1)} %bitcast.60) | data formatting | bytes 16777216 | tf_op jit(solution)/shard_map/transpose | solution.py:50
  13.7 5.9 all-to-all-start
  19.6 0.1 fusion.39
  19.7 0.5 fusion.31
  20.2 0.0 copy-start.3
  20.3 0.0 copy-start.4
  20.3 180.7 %all-to-all-done = f32[2,32,256,128]{3,0,2,1:T(2,128)} async-done(((f32[2,32,256,128]{3,0,2,1:T(2,128)}), f32[2,32,256,128]{3,0,2,1:T(2,128)}, u32[]{:S(2)}, u32[]{:S(2)}) %all-to-all-start) | async-done | bytes 8388640 | tf_op jit(solution)/shard_map/all_to_all | solution.py:39
  201.0 0.0 copy-done.2
  201.0 12.1 %fusion.15 = f32[2,32,256,128]{3,1,2,0:T(8,128)S(1)} fusion(f32[2,32,2,32,1]{3,1,2,4,0:T(8,128)S(1)} %copy-done.2, f32[2,32,256,128]{3,0,2,1:T(2,128)} %all-to-all-done), kind=kOutput, calls=%fused_computation.24 | convolution fusion | flops 805306368 | bytes 16793600 | tf_op jit(solution)/shard_map/vkut,utab->vkab/dot_general | solution.py:13
  213.1 0.0 copy-done.3
  213.1 3.1 multiply_subtract_fusion.2
  216.3 0.0 copy-start
  216.3 1.0 pad_maximum_fusion
  217.3 0.2 copy-done
  217.5 11.0 %fusion.21 = f32[2,256,32,128]{3,1,2,0:T(8,128)S(1)} fusion(f32[2,256,2,256,1]{3,1,2,4,0:T(8,128)S(1)} %copy-done, f32[2,32,256,128]{3,1,2,0:T(8,128)S(1)} %pad_maximum_fusion), kind=kOutput, calls=%fused_computation.26 | convolution fusion | flops 6442450944 | bytes 17825792 | tf_op jit(solution)/shard_map/vkua,uqab->vkqb/dot_general | solution.py:13
  228.6 2.1 multiply_subtract_fusion.1
  230.6 2.4 copy.32
  233.1 2.4 copy.33
  235.5 1.0 pad_maximum_fusion.1
  236.5 31.5 %copy.34 = f32[2,32,256,128]{3,0,2,1:T(2,128)S(1)} copy(f32[2,32,256,128]{3,2,1,0:T(8,128)S(1)} %pad_maximum_fusion.1) | data formatting | bytes 16777216 | tf_op jit(solution)/shard_map/stack | solution.py:60
  268.1 195.6 %all_to_all.15 = f32[2,32,256,128]{3,0,2,1:T(2,128)S(1)} all-to-all(f32[2,32,256,128]{3,0,2,1:T(2,128)S(1)} %copy.34), channel_id=1, replica_groups=mesh['hi'=4,'lo'=8] {'hi','lo'}, dimensions={1} | all-to-all | bytes 16777216 | tf_op jit(solution)/shard_map/all_to_all | solution.py:39
  463.7 8.5 %fusion.18 = f32[2,32,256,128]{3,1,2,0:T(8,128)S(1)} fusion(f32[2,32,2,32,1]{3,1,2,4,0:T(8,128)S(1)} %copy-done.2, f32[2,32,256,128]{3,0,2,1:T(2,128)S(1)} %all_to_all.15), kind=kOutput, calls=%fused_computation.25 | convolution fusion | flops 805306368 | bytes 16793600 | tf_op jit(solution)/shard_map/vkud,udqb->vkqb/dot_general | solution.py:13
  472.3 1.3 multiply_subtract_fusion
  473.6 0.0 copy-start.1
  473.6 1.0 pad_maximum_fusion.2
  474.6 8.5 %fusion.12 = f32[2,128,32,256]{3,1,2,0:T(8,128)S(1)} fusion(f32[2,128,2,128,1]{3,1,2,4,0:T(8,128)S(1)} %copy-done.1, f32[2,32,256,128]{3,1,2,0:T(8,128)S(1)} %pad_maximum_fusion.2), kind=kOutput, calls=%fused_computation.23 | convolution fusion | flops 3221225472 | bytes 17039360 | tf_op jit(solution)/shard_map/vkub,upqb->vkpq/dot_general | solution.py:13
  483.2 4.9 copy.37
  488.0 1.0 copy.38
  489.0 192.9 %all_to_all.16 = f32[2,32,128,256]{3,2,0,1:T(8,128)S(1)} all-to-all(f32[2,32,128,256]{3,2,0,1:T(8,128)S(1)} %copy.38), channel_id=1, replica_groups=mesh['hi'=4,'lo'=8] {'hi','lo'}, dimensions={1} | all-to-all | bytes 16777216 | tf_op jit(solution)/shard_map/all_to_all | solution.py:39
  681.9 4.9 copy.39
  686.8 23.4 %copy.48 = f32[1,2,4096,256]{3,1,2,0:T(2,128)} copy(f32[1,2,4096,256]{3,2,1,0:T(8,128)S(1)} %bitcast.59) | data formatting | bytes 16777216
  (8 shorter events, 0.0 us)
Async XLA Ops:
  13.7 187.3 %copy-start.2 = (f32[2,32,2,32,1]{3,1,2,4,0:T(8,128)S(1)}, f32[2,32,2,32,1]{3,1,2,4,0:T(8,128)}, u32[]{:S(2)}) copy-start(f32[2,32,2,32,1]{3,1,2,4,0:T(8,128)} %constant.71) | copy-start | bytes 49156
  13.7 187.3 %all-to-all-start = ((f32[2,32,256,128]{3,0,2,1:T(2,128)}), f32[2,32,256,128]{3,0,2,1:T(2,128)}, u32[]{:S(2)}, u32[]{:S(2)}) async-start(f32[2,32,256,128]{3,0,2,1:T(2,128)} %copy.29), calls=%async_computation | async-start | bytes 16777216 | tf_op jit(solution)/shard_map/all_to_all | solution.py:39
  20.2 192.9 %copy-start.3 = (f32[32,256]{0,1:T(8,128)S(1)}, f32[32,256]{0,1:T(8,128)}, u32[]{:S(2)}) copy-start(f32[32,256]{0,1:T(8,128)} %constant.66) | copy-start | bytes 98308
  20.3 192.9 %copy-start.4 = (f32[32,256]{0,1:T(8,128)S(1)}, f32[32,256]{0,1:T(8,128)}, u32[]{:S(2)}) copy-start(f32[32,256]{0,1:T(8,128)} %constant.67) | copy-start | bytes 98308
  216.3 1.2 copy-start
  463.7 8.6 %copy-start.5 = (f32[32,128]{1,0:T(8,128)S(1)}, f32[32,128]{1,0:T(8,128)}, u32[]{:S(2)}) copy-start(f32[32,128]{1,0:T(8,128)} %constant.68) | copy-start | bytes 49156
  463.7 8.6 %copy-start.6 = (f32[32,128]{1,0:T(8,128)S(1)}, f32[32,128]{1,0:T(8,128)}, u32[]{:S(2)}) copy-start(f32[32,128]{1,0:T(8,128)} %constant.69) | copy-start | bytes 49156
  473.6 1.0 copy-start.1

commit v2 on v1

--- a/solution.py
+++ b/solution.py
@@ -1,9 +1,12 @@
+import functools
 import math
 
 import jax
 import jax.numpy as jnp
 import numpy as np
 from jax import lax
+from jax.experimental import pallas as pl
+from jax.experimental.pallas import tpu as pltpu
 from jax.sharding import PartitionSpec as P
 
 LANES = 128
@@ -37,6 +40,140 @@
 
 def swap(blocks):
     return lax.all_to_all(blocks, ("hi", "lo"), split_axis=1, concat_axis=1, tiled=True)
+
+
+def halves(value):
+    high = value.astype(jnp.bfloat16)
+    return high, (value - high.astype(jnp.float32)).astype(jnp.bfloat16)
+
+
+def table_halves(length):
+    table = dft_table(length).reshape(2 * length, 2 * length)
+    high = table.astype(jnp.bfloat16)
+    low = (table - high.astype(np.float32)).astype(jnp.bfloat16)
+    return np.concatenate([high, high, low], axis=1)
+
+
+def mix(table, data):
+    high, low = halves(data)
+    parts = jnp.concatenate([high, low, high], axis=0)
+    return jnp.dot(table, parts, preferred_element_type=jnp.float32)
+
+
+def call(kernel, shape, *operands, scratch=()):
+    return pl.pallas_call(
+        kernel,
+        out_shape=jax.ShapeDtypeStruct(shape, jnp.float32),
+        scratch_shapes=[pltpu.VMEM(s, jnp.float32) for s in scratch],
+        compiler_params=pltpu.CompilerParams(vmem_limit_bytes=60 * 2**20),
+    )(*operands)
+
+
+def entry_kernel(count, mid, x_ref, o_ref):
+    @pl.loop(0, count)
+    def _(d):
+        for u in range(2):
+            o_ref[pl.ds((u * count + d) * mid, mid), :] = x_ref[pl.ds(d * 2 + u, mid, stride=2 * count), :]
+
+
+def first_kernel(count, mid, x_ref, t1_ref, t2_ref, own_ref, rest_ref, turn_ref, z_ref, y_ref):
+    low = count * mid
+
+    @pl.loop(0, mid // 8)
+    def _(c):
+        cols = []
+        for i in range(8):
+            cols.append(jnp.concatenate([x_ref[pl.ds(u * low + c * 8 + i, count, stride=mid), :] for u in range(2)], axis=0))
+        out = mix(t1_ref[...], jnp.concatenate(cols, axis=1))
+        rest = (rest_ref[0], rest_ref[1])
+        for i in range(8):
+            own = (own_ref[0, c, :, i : i + 1], own_ref[1, c, :, i : i + 1])
+            mine = out[:, i * LANES : (i + 1) * LANES]
+            got = times(times((mine[:count], mine[count:]), own), rest)
+            for u in range(2):
+                y_ref[pl.ds(u * low + c * 8 + i, count, stride=mid), :] = got[u]
+
+    @pl.loop(0, count // 2)
+    def _(c):
+        cols = []
+        for i in range(2):
+            cols.append(jnp.concatenate([y_ref[pl.ds(u * low + (c * 2 + i) * mid, mid), :] for u in range(2)], axis=0))
+        out = mix(t2_ref[...], jnp.concatenate(cols, axis=1))
+        turn = (turn_ref[0], turn_ref[1])
+        for i in range(2):
+            mine = out[:, i * LANES : (i + 1) * LANES]
+            got = times((mine[:mid], mine[mid:]), turn)
+            for u in range(2):
+                z_ref[pl.ds(u * low + c * 2 + i, mid, stride=count), :] = got[u]
+
+
+def second_kernel(count, mid, x_ref, t3_ref, t4_ref, turn_ref, o_ref, s_ref):
+    low = count * mid
+    pages = mid // LANES
+
+    @pl.loop(0, mid // 8)
+    def _(c):
+        cols = []
+        for i in range(8):
+            cols.append(jnp.concatenate([x_ref[pl.ds(u * low + c * 8 + i, count, stride=mid), :] for u in range(2)], axis=0))
+        out = mix(t3_ref[...], jnp.concatenate(cols, axis=1))
+        turn = (turn_ref[0], turn_ref[1])
+        for i in range(8):
+            mine = out[:, i * LANES : (i + 1) * LANES]
+            got = times((mine[:count], mine[count:]), turn)
+            for u in range(2):
+                s_ref[pl.ds(u * low + c * 8 + i, count, stride=mid), :] = got[u]
+
+    @pl.loop(0, count)
+    def _(k2):
+        high, lows = halves(jnp.concatenate([s_ref[pl.ds(u * low + k2 * mid, mid), :] for u in range(2)], axis=1))
+        parts = jnp.concatenate([high, lows, high], axis=1)
+        out = lax.dot_general(t4_ref[...], parts, (((1,), (1,)), ((), ())), preferred_element_type=jnp.float32)
+        for v in range(2):
+            for h in range(pages):
+                o_ref[pl.ds(v * LANES * count * pages + k2 * pages + h, LANES, stride=count * pages), :] = out[
+                    v * LANES : (v + 1) * LANES, h * LANES : (h + 1) * LANES
+                ]
+
+
+def final_kernel(count, mid, x_ref, o_ref):
+    pages = mid // LANES
+
+    @pl.loop(0, count)
+    def _(s):
+        for v in range(2):
+            for h in range(pages):
+                o_ref[pl.ds((s * pages + h) * 2 + v, LANES, stride=count * pages * 2), :] = x_ref[
+                    pl.ds((v * count + s) * LANES * pages + h, LANES, stride=pages), :
+                ]
+
+
+def shards_by_kernels(state, count, me):
+    amplitudes = state.shape[1]
+    whole = amplitudes * count
+    mid = amplitudes // (count * LANES)
+    low = count * mid
+    rows = (2 * low, LANES)
+    bind = functools.partial
+    x = state.reshape(2, low, LANES).transpose(1, 0, 2).reshape(rows)
+    x = call(bind(entry_kernel, count, mid), rows, x)
+    x = swap(x.reshape(2, count, mid, LANES)).reshape(rows)
+    places = me * LANES + jnp.arange(LANES, dtype=jnp.int32)
+    rest = jnp.stack(unit(jnp.arange(count, dtype=jnp.int32)[:, None] * places[None, :], whole))
+    turn = jnp.stack(unit(jnp.arange(mid, dtype=jnp.int32)[:, None] * places[None, :], whole // count))
+    own = jnp.asarray(np.stack(fixed_unit(count, mid, low)))
+    own = own.reshape(2, count, mid // 8, 8).transpose(0, 2, 1, 3)
+    x = call(
+        bind(first_kernel, count, mid), rows, x, table_halves(count), table_halves(mid), own, rest, turn, scratch=(rows,)
+    )
+    x = swap(x.reshape(2, count, mid, LANES)).reshape(rows)
+    turn = jnp.asarray(np.stack(fixed_unit(count, LANES, count * LANES)))
+    x = call(
+        bind(second_kernel, count, mid), rows, x, table_halves(count), table_halves(LANES), turn, scratch=(rows,)
+    )
+    x = swap(x.reshape(2, count, mid, LANES)).reshape(rows)
+    x = call(bind(final_kernel, count, mid), rows, x)
+    return x.reshape(low, 2, LANES).transpose(1, 0, 2).reshape(2, amplitudes)
 
 
 def shards(state):
@@ -47,6 +184,8 @@
     whole = amplitudes * count
     mid = amplitudes // (count * LANES)
     low = count * mid
+    if mid % LANES == 0 and LANES % count == 0 and count % 8 == 0:
+        return shards_by_kernels(state, count, me)
     blocks = state.reshape(2, mid, count, LANES).transpose(0, 2, 1, 3)
     x = swap(blocks)
     x = product("vkut,utab->vkab", dft_table(count), x)

time: 717 us -> 713 us (level)
  Pallas kernels: 0 us -> 106 us
  local copies, waits for them, and re-layouts: 84.4 us -> 30.9 us
  matrix products: 40.2 us -> 0 us
  other arithmetic: 10.2 us -> 1.96 us
    pallas_call x0 -> x4, Pallas kernels: none -> 106 us  [call(): pl.pallas_call(kernel, out_shape=jax.ShapeDtypeStruct(shape, jnp.float32)...]
    dot_general x4 -> x0, matrix products: 40.2 us -> none  [product(): jnp.einsum(spec, left, right, precision=lax.Precision.HIGH, preferred_ele...]
    another operation x1 -> x0, local copies, waits for them, and re-layouts: 31.5 us -> none  [shards(): jnp.stack(times((x[0], x[1]), (turn[0][:, None, :], turn[1][:, None, :])))]
    unnamed x16 -> x0, local copies, waits for them, and re-layouts: 27.6 us -> none
    all_to_all x0 -> x3, local copies, waits for them, and re-layouts: none -> 15.5 us  [swap(): lax.all_to_all(blocks, ('hi', 'lo'), split_axis=1, concat_axis=1, tiled=T...]
    transpose x2 -> x0, local copies, waits for them, and re-layouts: 14.6 us -> none  [the longest x1 9.75 us: shards(): blocks = state.reshape(2, mid, count, LANES).transpose(0, 2, 1, 3)]
    reshape x1 -> x3, local copies, waits for them, and re-layouts: 0.98 us -> 15.4 us  [shards_by_kernels(): x = swap(x.reshape(2, count, mid, LANES)).reshape(rows)]
where the time goes in v2:
time: 713 us
  blocking collectives  389 us (55%)
  waiting for transfers between devices  179 us (25%)
  Pallas kernels  106 us (15%)
  local copies, waits for them, and re-layouts  30.9 us (4%)
    all_to_all x2, blocking collectives, swap(): lax.all_to_all(blocks, ('hi', 'lo'), split_axis=1, concat_axis=1, tiled=T...  389 us
    all_to_all x1, waiting for transfers between devices, swap(): lax.all_to_all(blocks, ('hi', 'lo'), split_axis=1, concat_axis=1, tiled=T...  179 us
    pallas_call x4, Pallas kernels, call(): pl.pallas_call(kernel, out_shape=jax.ShapeDtypeStruct(shape, jnp.float32)...  106 us
    all_to_all x3, local copies, waits for them, and re-layouts, swap(): lax.all_to_all(blocks, ('hi', 'lo'), split_axis=1, concat_axis=1, tiled=T...  15.5 us
    reshape x3, local copies, waits for them, and re-layouts, shards_by_kernels(): x = swap(x.reshape(2, count, mid, LANES)).reshape(rows)  15.4 us
  transfers between devices with their start and end apart: 1, of which 1 were waited for; matrix products, arithmetic and copies ran while one was open for 0% of the time, Pallas kernels for 0%

profile of v2, /device:TPU:24, one launch (start us, length us, event | category | flops | bytes accessed | tf_op | source)
XLA Modules:
  0.0 712.8 jit_solution(8522143642507472806)
XLA Ops:
  0.0 15.0 %shard_map.73 = f32[16384,128]{1,0:T(8,128)} custom-call(f32[16384,128]{1,0:T(8,128)} %bitcast.22), custom_call_target="tpu_custom_call" | custom-call | tf_op jit(solution)/shard_map/pallas_call | solution.py:64
  15.0 7.6 %copy.11 = f32[2,32,256,128]{3,2,0,1:T(8,128)} copy(f32[2,32,256,128]{3,2,1,0:T(8,128)} %bitcast.21) | data formatting | bytes 16777216 | tf_op jit(solution)/shard_map/reshape | solution.py:160
  22.6 5.9 all-to-all-start
  28.5 0.1 fusion.15
  28.6 0.6 pad_maximum_fusion.1.rest_ref
  29.3 0.5 fusion.7
  29.8 0.7 pad_maximum_fusion.turn_ref
  30.5 179.4 %all-to-all-done = f32[2,32,256,128]{3,2,0,1:T(8,128)} async-done(((f32[2,32,256,128]{3,2,0,1:T(8,128)}), f32[2,32,256,128]{3,2,0,1:T(8,128)}, u32[]{:S(2)}, u32[]{:S(2)}) %all-to-all-start) | async-done | bytes 8388640 | tf_op jit(solution)/shard_map/all_to_all | solution.py:42
  209.9 7.8 %copy.12 = f32[2,32,256,128]{3,2,1,0:T(8,128)} copy(f32[2,32,256,128]{3,2,0,1:T(8,128)} %all-to-all-done) | data formatting | bytes 16777216 | tf_op jit(solution)/shard_map/all_to_all | solution.py:42
  217.7 38.5 %shard_map.74 = f32[16384,128]{1,0:T(8,128)} custom-call(f32[16384,128]{1,0:T(8,128)} %bitcast.16, bf16[64,192]{1,0:T(8,128)(2,1)} %constant.56.clone.t1_ref.t3_ref, bf16[512,1536]{1,0:T(8,128)(2,1)} %constant.57.clone.t2_ref, f32[2,32,32,8]{3,2,1,0:T(8,128)} %constant.61.own_ref, f32[2,32,128]{2,1,0:T(8,128)} %pad_maximum_fusion.1.rest_ref, ...), custom_call_target="tpu_custom_call" | custom-call | tf_op jit(solution)/shard_map/pallas_call | solution.py:64
  256.2 3.9 copy.13
  260.2 195.6 %all_to_all.15 = f32[2,32,256,128]{3,2,0,1:T(8,128)S(1)} all-to-all(f32[2,32,256,128]{3,2,0,1:T(8,128)S(1)} %copy.13), channel_id=1, replica_groups=mesh['hi'=4,'lo'=8] {'hi','lo'}, dimensions={1} | all-to-all | bytes 16777216 | tf_op jit(solution)/shard_map/all_to_all | solution.py:42
  455.8 3.9 copy.14
  459.7 37.1 %shard_map.75 = f32[16384,128]{1,0:T(8,128)} custom-call(f32[16384,128]{1,0:T(8,128)} %bitcast.18, bf16[64,192]{1,0:T(8,128)(2,1)} %constant.56.clone.t1_ref.t3_ref, bf16[256,768]{1,0:T(8,128)(2,1)} %constant.59.clone.t4_ref, f32[2,32,128]{2,1,0:T(8,128)} %constant.58.clone.turn_ref), custom_call_target="tpu_custom_call" | custom-call | tf_op jit(solution)/shard_map/pallas_call | solution.py:64
  496.8 3.9 copy.15
  500.8 192.9 %all_to_all.16 = f32[2,32,256,128]{3,2,0,1:T(8,128)S(1)} all-to-all(f32[2,32,256,128]{3,2,0,1:T(8,128)S(1)} %copy.15), channel_id=1, replica_groups=mesh['hi'=4,'lo'=8] {'hi','lo'}, dimensions={1} | all-to-all | bytes 16777216 | tf_op jit(solution)/shard_map/all_to_all | solution.py:42
  693.6 3.8 copy.16
  697.4 15.4 %shard_map.76 = f32[16384,128]{1,0:T(8,128)} custom-call(f32[16384,128]{1,0:T(8,128)} %bitcast.20), custom_call_target="tpu_custom_call" | custom-call | tf_op jit(solution)/shard_map/pallas_call | solution.py:64
  (1 shorter events, 0.0 us)
Async XLA Ops:
  22.6 187.3 %all-to-all-start = ((f32[2,32,256,128]{3,2,0,1:T(8,128)}), f32[2,32,256,128]{3,2,0,1:T(8,128)}, u32[]{:S(2)}, u32[]{:S(2)}) async-start(f32[2,32,256,128]{3,2,0,1:T(8,128)} %copy.11), calls=%async_computation | async-start | bytes 16777216 | tf_op jit(solution)/shard_map/all_to_all | solution.py:42

commit v3 on v2

--- a/solution.py
+++ b/solution.py
@@ -38,8 +38,8 @@
     return (left[0] * right[0] - left[1] * right[1], left[0] * right[1] + left[1] * right[0])
 
 
-def swap(blocks):
-    return lax.all_to_all(blocks, ("hi", "lo"), split_axis=1, concat_axis=1, tiled=True)
+def swap(blocks, axis=1):
+    return lax.all_to_all(blocks, ("hi", "lo"), split_axis=axis, concat_axis=axis, tiled=True)
 
 
 def halves(value):
@@ -69,21 +69,25 @@
     )(*operands)
 
 
-def entry_kernel(count, mid, x_ref, o_ref):
-    @pl.loop(0, count)
+STEPS = 4
+
+
+def entry_kernel(count, x_ref, o_ref):
+    @pl.loop(0, count, unroll=2)
     def _(d):
         for u in range(2):
-            o_ref[pl.ds((u * count + d) * mid, mid), :] = x_ref[pl.ds(d * 2 + u, mid, stride=2 * count), :]
+            o_ref[d * 2 + u] = x_ref[pl.ds(d * 2 + u, o_ref.shape[1], stride=2 * count), :]
 
 
 def first_kernel(count, mid, x_ref, t1_ref, t2_ref, own_ref, rest_ref, turn_ref, z_ref, y_ref):
     low = count * mid
-
-    @pl.loop(0, mid // 8)
+    run = mid // count
+
+    @pl.loop(0, mid // 8, unroll=2)
     def _(c):
         cols = []
         for i in range(8):
-            cols.append(jnp.concatenate([x_ref[pl.ds(u * low + c * 8 + i, count, stride=mid), :] for u in range(2)], axis=0))
+            cols.append(jnp.concatenate([x_ref[pl.ds(u * mid + c * 8 + i, count, stride=2 * mid), :] for u in range(2)], axis=0))
         out = mix(t1_ref[...], jnp.concatenate(cols, axis=1))
         rest = (rest_ref[0], rest_ref[1])
         for i in range(8):
@@ -93,7 +97,7 @@
             for u in range(2):
                 y_ref[pl.ds(u * low + c * 8 + i, count, stride=mid), :] = got[u]
 
-    @pl.loop(0, count // 2)
+    @pl.loop(0, count // 2, unroll=2)
     def _(c):
         cols = []
         for i in range(2):
@@ -103,48 +107,54 @@
         for i in range(2):
             mine = out[:, i * LANES : (i + 1) * LANES]
             got = times((mine[:mid], mine[mid:]), turn)
-            for u in range(2):
-                z_ref[pl.ds(u * low + c * 2 + i, mid, stride=count), :] = got[u]
+            for d in range(count):
+                for u in range(2):
+                    z_ref[pl.ds((d * 2 + u) * mid + (c * 2 + i) * run, run), :] = got[u][d * run : (d + 1) * run]
 
 
 def second_kernel(count, mid, x_ref, t3_ref, t4_ref, turn_ref, o_ref, s_ref):
     low = count * mid
     pages = mid // LANES
-
-    @pl.loop(0, mid // 8)
+    run = mid // count
+    tops = LANES // count
+
+    @pl.loop(0, count, unroll=2)
     def _(c):
         cols = []
-        for i in range(8):
-            cols.append(jnp.concatenate([x_ref[pl.ds(u * low + c * 8 + i, count, stride=mid), :] for u in range(2)], axis=0))
+        for i in range(run):
+            cols.append(jnp.concatenate([x_ref[pl.ds(u * mid + c * run + i, count, stride=2 * mid), :] for u in range(2)], axis=0))
         out = mix(t3_ref[...], jnp.concatenate(cols, axis=1))
         turn = (turn_ref[0], turn_ref[1])
-        for i in range(8):
+        for i in range(run):
             mine = out[:, i * LANES : (i + 1) * LANES]
             got = times((mine[:count], mine[count:]), turn)
             for u in range(2):
-                s_ref[pl.ds(u * low + c * 8 + i, count, stride=mid), :] = got[u]
-
-    @pl.loop(0, count)
+                s_ref[pl.ds(u * low + i * count + c, count, stride=mid), :] = got[u]
+
+    @pl.loop(0, count, unroll=2)
     def _(k2):
         high, lows = halves(jnp.concatenate([s_ref[pl.ds(u * low + k2 * mid, mid), :] for u in range(2)], axis=1))
         parts = jnp.concatenate([high, lows, high], axis=1)
         out = lax.dot_general(t4_ref[...], parts, (((1,), (1,)), ((), ())), preferred_element_type=jnp.float32)
-        for v in range(2):
-            for h in range(pages):
-                o_ref[pl.ds(v * LANES * count * pages + k2 * pages + h, LANES, stride=count * pages), :] = out[
-                    v * LANES : (v + 1) * LANES, h * LANES : (h + 1) * LANES
-                ]
+        for top in range(tops):
+            for v in range(2):
+                start = (v * tops + top) * count * pages
+                for h in range(pages):
+                    o_ref[pl.ds(start + k2 * pages + h, count, stride=2 * mid), :] = out[
+                        (top * 2 + v) * count : (top * 2 + v + 1) * count, h * LANES : (h + 1) * LANES
+                    ]
 
 
 def final_kernel(count, mid, x_ref, o_ref):
     pages = mid // LANES
-
-    @pl.loop(0, count)
+    part = x_ref.shape[1] // pages
+
+    @pl.loop(0, count, unroll=2)
     def _(s):
         for v in range(2):
             for h in range(pages):
-                o_ref[pl.ds((s * pages + h) * 2 + v, LANES, stride=count * pages * 2), :] = x_ref[
-                    pl.ds((v * count + s) * LANES * pages + h, LANES, stride=pages), :
+                o_ref[pl.ds((s * pages + h) * 2 + v, part, stride=count * pages * 2), :] = x_ref[
+                    s * 2 + v, pl.ds(h, part, stride=pages), :
                 ]
 
 
@@ -154,10 +164,16 @@
     mid = amplitudes // (count * LANES)
     low = count * mid
     rows = (2 * low, LANES)
+    blocks = (2 * count, mid, LANES)
+    flat_spec = pl.BlockSpec((2 * low // STEPS, LANES), lambda g: (g, 0))
+    block_spec = pl.BlockSpec((2 * count, mid // STEPS, LANES), lambda g: (0, g, 0))
     bind = functools.partial
     x = state.reshape(2, low, LANES).transpose(1, 0, 2).reshape(rows)
-    x = call(bind(entry_kernel, count, mid), rows, x)
-    x = swap(x.reshape(2, count, mid, LANES)).reshape(rows)
+    x = pl.pallas_call(
+        bind(entry_kernel, count), out_shape=jax.ShapeDtypeStruct(blocks, jnp.float32),
+        grid=(STEPS,), in_specs=[flat_spec], out_specs=block_spec,
+    )(x)
+    x = swap(x.reshape(count, 2 * mid, LANES), 0).reshape(rows)
     places = me * LANES + jnp.arange(LANES, dtype=jnp.int32)
     rest = jnp.stack(unit(jnp.arange(count, dtype=jnp.int32)[:, None] * places[None, :], whole))
     turn = jnp.stack(unit(jnp.arange(mid, dtype=jnp.int32)[:, None] * places[None, :], whole // count))
@@ -166,13 +182,16 @@
     x = call(
         bind(first_kernel, count, mid), rows, x, table_halves(count), table_halves(mid), own, rest, turn, scratch=(rows,)
     )
-    x = swap(x.reshape(2, count, mid, LANES)).reshape(rows)
+    x = swap(x.reshape(count, 2 * mid, LANES), 0).reshape(rows)
     turn = jnp.asarray(np.stack(fixed_unit(count, LANES, count * LANES)))
-    x = call(
-        bind(second_kernel, count, mid), rows, x, table_halves(count), table_halves(LANES), turn, scratch=(rows,)
-    )
-    x = swap(x.reshape(2, count, mid, LANES)).reshape(rows)
-    x = call(bind(final_kernel, count, mid), rows, x)
+    t4 = table_halves(LANES)
+    t4 = t4.reshape(2, count, LANES // count, -1).transpose(2, 0, 1, 3).reshape(t4.shape)
+    x = call(bind(second_kernel, count, mid), rows, x, table_halves(count), t4, turn, scratch=(rows,))
+    x = swap(x.reshape(count, 2 * mid, LANES), 0).reshape(blocks)
+    x = pl.pallas_call(
+        bind(final_kernel, count, mid), out_shape=jax.ShapeDtypeStruct(rows, jnp.float32),
+        grid=(STEPS,), in_specs=[block_spec], out_specs=flat_spec,
+    )(x)
     return x.reshape(low, 2, LANES).transpose(1, 0, 2).reshape(2, amplitudes)
 
 
@@ -184,7 +203,7 @@
     whole = amplitudes * count
     mid = amplitudes // (count * LANES)
     low = count * mid
-    if mid % LANES == 0 and LANES % count == 0 and count % 8 == 0:
+    if mid % LANES == 0 and LANES % count == 0 and count % 8 == 0 and mid % (8 * count) == 0:
         return shards_by_kernels(state, count, me)
     blocks = state.reshape(2, mid, count, LANES).transpose(0, 2, 1, 3)
     x = swap(blocks)

time: 713 us -> 657 us (0.921)
  local copies, waits for them, and re-layouts: 30.9 us -> 0 us
  Pallas kernels: 106 us -> 82.1 us
    pallas_call x4 -> x2, Pallas kernels: 106 us -> 61 us  [call(): pl.pallas_call(kernel, out_shape=jax.ShapeDtypeStruct(shape, jnp.float32)...]
    pallas_call x0 -> x2, Pallas kernels: none -> 21.1 us  [the longest x1 11.2 us: shards_by_kernels(): pl.pallas_call(bind(final_kernel, count, mid), out_shape=jax.ShapeDtypeSt...]
    all_to_all x3 -> x0, local copies, waits for them, and re-layouts: 15.5 us -> none  [swap(): lax.all_to_all(blocks, ('hi', 'lo'), split_axis=1, concat_axis=1, tiled=T...]
    reshape x3 -> x0, local copies, waits for them, and re-layouts: 15.4 us -> none  [shards_by_kernels(): x = swap(x.reshape(2, count, mid, LANES)).reshape(rows)]
where the time goes in v3:
time: 657 us; the launch traced here: 655 us
  blocking collectives  385 us (59%)
  waiting for transfers between devices  179 us (27%)
  Pallas kernels  82.1 us (12%)
    all_to_all x2, blocking collectives, swap(): lax.all_to_all(blocks, ('hi', 'lo'), split_axis=axis, concat_axis=axis, t...  385 us
    all_to_all x1, waiting for transfers between devices, swap(): lax.all_to_all(blocks, ('hi', 'lo'), split_axis=axis, concat_axis=axis, t...  179 us
    pallas_call x2, Pallas kernels, call(): pl.pallas_call(kernel, out_shape=jax.ShapeDtypeStruct(shape, jnp.float32)...  61 us
  transfers between devices with their start and end apart: 1, of which 1 were waited for; matrix products, arithmetic and copies ran while one was open for 0% of the time, Pallas kernels for 0%

profile of v3, /device:TPU:24, one launch (start us, length us, event | category | flops | bytes accessed | tf_op | source)
XLA Modules:
  0.0 654.7 jit_solution(14568936795999143071)
XLA Ops:
  0.0 9.8 %shard_map.73 = f32[64,256,128]{2,1,0:T(8,128)} custom-call(f32[16384,128]{1,0:T(8,128)} %bitcast.21), custom_call_target="tpu_custom_call" | custom-call | tf_op jit(solution)/shard_map/pallas_call | solution.py:172
  9.9 5.9 all-to-all-start
  15.8 0.1 fusion.15
  15.9 0.6 pad_maximum_fusion.1.rest_ref
  16.5 0.5 fusion.7
  17.0 0.7 pad_maximum_fusion.turn_ref
  17.8 179.4 %all-to-all-done = f32[32,512,128]{2,1,0:T(8,128)} async-done(((f32[32,512,128]{2,1,0:T(8,128)}), f32[32,512,128]{2,1,0:T(8,128)}, u32[]{:S(2)}, u32[]{:S(2)}) %all-to-all-start) | async-done | bytes 8388640 | tf_op jit(solution)/shard_map/all_to_all | solution.py:42
  197.2 29.2 %shard_map.74 = f32[16384,128]{1,0:T(8,128)} custom-call(f32[16384,128]{1,0:T(8,128)} %bitcast.4.x_ref, bf16[64,192]{1,0:T(8,128)(2,1)} %constant.56.clone.t1_ref.t3_ref, bf16[512,1536]{1,0:T(8,128)(2,1)} %constant.57.clone.t2_ref, f32[2,32,32,8]{3,2,1,0:T(8,128)} %constant.61.own_ref, f32[2,32,128]{2,1,0:T(8,128)} %pad_maximum_fusion.1.rest_ref, ...), custom_call_target="tpu_custom_call" | custom-call | tf_op jit(solution)/shard_map/pallas_call | solution.py:64
  226.4 193.5 %all_to_all.15 = f32[32,512,128]{2,1,0:T(8,128)} all-to-all(f32[32,512,128]{2,1,0:T(8,128)} %bitcast.16), channel_id=1, replica_groups=mesh['hi'=4,'lo'=8] {'hi','lo'}, dimensions={0} | all-to-all | bytes 16777216 | tf_op jit(solution)/shard_map/all_to_all | solution.py:42
  419.9 31.8 %shard_map.75 = f32[16384,128]{1,0:T(8,128)} custom-call(f32[16384,128]{1,0:T(8,128)} %bitcast.18, bf16[64,192]{1,0:T(8,128)(2,1)} %constant.56.clone.t1_ref.t3_ref, bf16[256,768]{1,0:T(8,128)(2,1)} %constant.59.clone.t4_ref, f32[2,32,128]{2,1,0:T(8,128)} %constant.58.clone.turn_ref), custom_call_target="tpu_custom_call" | custom-call | tf_op jit(solution)/shard_map/pallas_call | solution.py:64
  451.7 191.8 %all_to_all.16 = f32[32,512,128]{2,1,0:T(8,128)} all-to-all(f32[32,512,128]{2,1,0:T(8,128)} %bitcast.19), channel_id=1, replica_groups=mesh['hi'=4,'lo'=8] {'hi','lo'}, dimensions={0} | all-to-all | bytes 16777216 | tf_op jit(solution)/shard_map/all_to_all | solution.py:42
  643.5 11.2 %shard_map.76 = f32[16384,128]{1,0:T(8,128)} custom-call(f32[64,256,128]{2,1,0:T(8,128)} %bitcast.20), custom_call_target="tpu_custom_call" | custom-call | tf_op jit(solution)/shard_map/pallas_call | solution.py:191
  (1 shorter events, 0.0 us)
Async XLA Ops:
  9.9 187.3 %all-to-all-start = ((f32[32,512,128]{2,1,0:T(8,128)}), f32[32,512,128]{2,1,0:T(8,128)}, u32[]{:S(2)}, u32[]{:S(2)}) async-start(f32[32,512,128]{2,1,0:T(8,128)} %bitcast.17), calls=%async_computation | async-start | bytes 16777216 | tf_op jit(solution)/shard_map/all_to_all | solution.py:42

commit v4 on v3

--- a/solution.py
+++ b/solution.py
@@ -63,8 +63,9 @@
 def call(kernel, shape, *operands, scratch=()):
     return pl.pallas_call(
         kernel,
-        out_shape=jax.ShapeDtypeStruct(shape, jnp.float32),
+        out_shape=[jax.ShapeDtypeStruct(one, jnp.float32) for one in shape],
         scratch_shapes=[pltpu.VMEM(s, jnp.float32) for s in scratch],
+        cost_estimate=pl.CostEstimate(flops=8 * 10**9, bytes_accessed=2**24, transcendentals=0),
         compiler_params=pltpu.CompilerParams(vmem_limit_bytes=60 * 2**20),
     )(*operands)
 
@@ -79,9 +80,8 @@
             o_ref[d * 2 + u] = x_ref[pl.ds(d * 2 + u, o_ref.shape[1], stride=2 * count), :]
 
 
-def first_kernel(count, mid, x_ref, t1_ref, t2_ref, own_ref, rest_ref, turn_ref, z_ref, y_ref):
-    low = count * mid
-    run = mid // count
+def first_kernel(count, mid, x_ref, t1_ref, t2_ref, own_ref, rest_ref, turn_ref, y_ref, z_ref):
+    low = count * mid
 
     @pl.loop(0, mid // 8, unroll=2)
     def _(c):
@@ -97,6 +97,14 @@
             for u in range(2):
                 y_ref[pl.ds(u * low + c * 8 + i, count, stride=mid), :] = got[u]
 
+    page_kernel(count, mid, y_ref, t2_ref, turn_ref, z_ref)
+
+
+def page_kernel(count, mid, y_ref, t2_ref, turn_ref, z_ref):
+    low = count * mid
+    half = mid // 2
+    run = half // count
+
     @pl.loop(0, count // 2, unroll=2)
     def _(c):
         cols = []
@@ -104,12 +112,15 @@
             cols.append(jnp.concatenate([y_ref[pl.ds(u * low + (c * 2 + i) * mid, mid), :] for u in range(2)], axis=0))
         out = mix(t2_ref[...], jnp.concatenate(cols, axis=1))
         turn = (turn_ref[0], turn_ref[1])
+        got = []
         for i in range(2):
             mine = out[:, i * LANES : (i + 1) * LANES]
-            got = times((mine[:mid], mine[mid:]), turn)
-            for d in range(count):
-                for u in range(2):
-                    z_ref[pl.ds((d * 2 + u) * mid + (c * 2 + i) * run, run), :] = got[u][d * run : (d + 1) * run]
+            got.append(times((mine[:half], mine[half:]), turn))
+        for d in range(count):
+            for u in range(2):
+                z_ref[pl.ds((d * 2 + u) * half + c * 2 * run, 2 * run), :] = jnp.concatenate(
+                    [got[i][u][d * run : (d + 1) * run] for i in range(2)], axis=0
+                )
 
 
 def second_kernel(count, mid, x_ref, t3_ref, t4_ref, turn_ref, o_ref, s_ref):
@@ -145,17 +156,14 @@
                     ]
 
 
-def final_kernel(count, mid, x_ref, o_ref):
-    pages = mid // LANES
-    part = x_ref.shape[1] // pages
+def final_kernel(count, x0_ref, x1_ref, o_ref):
+    part = x0_ref.shape[1]
 
     @pl.loop(0, count, unroll=2)
     def _(s):
         for v in range(2):
-            for h in range(pages):
-                o_ref[pl.ds((s * pages + h) * 2 + v, part, stride=count * pages * 2), :] = x_ref[
-                    s * 2 + v, pl.ds(h, part, stride=pages), :
-                ]
+            for h, x_ref in enumerate((x0_ref, x1_ref)):
+                o_ref[pl.ds((s * 2 + h) * 2 + v, part, stride=count * 4), :] = x_ref[s * 2 + v]
 
 
 def shards_by_kernels(state, count, me):
@@ -179,19 +187,29 @@
     turn = jnp.stack(unit(jnp.arange(mid, dtype=jnp.int32)[:, None] * places[None, :], whole // count))
     own = jnp.asarray(np.stack(fixed_unit(count, mid, low)))
     own = own.reshape(2, count, mid // 8, 8).transpose(0, 2, 1, 3)
-    x = call(
-        bind(first_kernel, count, mid), rows, x, table_halves(count), table_halves(mid), own, rest, turn, scratch=(rows,)
-    )
-    x = swap(x.reshape(count, 2 * mid, LANES), 0).reshape(rows)
+    half = mid // 2
+    pages = (count, 2 * half, LANES)
+    flat = (2 * count * half, LANES)
+    t2 = table_halves(mid).reshape(2, count, 2, half // count, -1)
+    t2 = [t2[:, :, h].reshape(2 * half, -1) for h in range(2)]
+    turn = turn.reshape(2, count, 2, half // count, LANES)
+    turn = [turn[:, :, h].reshape(2, half, LANES) for h in range(2)]
+    y, z0 = call(bind(first_kernel, count, mid), (rows, flat), x, table_halves(count), t2[0], own, rest, turn[0])
+    z0 = swap(z0.reshape(pages), 0).reshape(flat)
+    (z1,) = call(bind(page_kernel, count, mid), (flat,), y, t2[1], turn[1])
+    z1 = swap(z1.reshape(pages), 0).reshape(flat)
     turn = jnp.asarray(np.stack(fixed_unit(count, LANES, count * LANES)))
     t4 = table_halves(LANES)
     t4 = t4.reshape(2, count, LANES // count, -1).transpose(2, 0, 1, 3).reshape(t4.shape)
-    x = call(bind(second_kernel, count, mid), rows, x, table_halves(count), t4, turn, scratch=(rows,))
-    x = swap(x.reshape(count, 2 * mid, LANES), 0).reshape(blocks)
+    done = []
+    for z in (z0, z1):
+        (z,) = call(bind(second_kernel, count, half), (flat,), z, table_halves(count), t4, turn, scratch=(flat,))
+        done.append(swap(z.reshape(pages), 0).reshape(2 * count, half, LANES))
+    page_spec = pl.BlockSpec((2 * count, half // STEPS, LANES), lambda g: (0, g, 0))
     x = pl.pallas_call(
-        bind(final_kernel, count, mid), out_shape=jax.ShapeDtypeStruct(rows, jnp.float32),
-        grid=(STEPS,), in_specs=[block_spec], out_specs=flat_spec,
-    )(x)
+        bind(final_kernel, count), out_shape=jax.ShapeDtypeStruct(rows, jnp.float32),
+        grid=(STEPS,), in_specs=[page_spec, page_spec], out_specs=flat_spec,
+    )(*done)
     return x.reshape(low, 2, LANES).transpose(1, 0, 2).reshape(2, amplitudes)
 
 
@@ -203,7 +221,7 @@
     whole = amplitudes * count
     mid = amplitudes // (count * LANES)
     low = count * mid
-    if mid % LANES == 0 and LANES % count == 0 and count % 8 == 0 and mid % (8 * count) == 0:
+    if mid == 2 * LANES and LANES % count == 0 and count % 8 == 0 and mid % (8 * count) == 0:
         return shards_by_kernels(state, count, me)
     blocks = state.reshape(2, mid, count, LANES).transpose(0, 2, 1, 3)
     x = swap(blocks)

time: 657 us -> 634 us (0.965)
  blocking collectives: 385 us -> 100 us
  waiting for transfers between devices: 179 us -> 399 us
  starting transfers between devices: 5.92 us -> 28.6 us
  Pallas kernels: 82.1 us -> 99.3 us
    all_to_all x2 -> x1, blocking collectives: 385 us -> 100 us  [swap(): lax.all_to_all(blocks, ('hi', 'lo'), split_axis=axis, concat_axis=axis, t...]
    all_to_all x1 -> x4, waiting for transfers between devices: 179 us -> 399 us  [swap(): lax.all_to_all(blocks, ('hi', 'lo'), split_axis=axis, concat_axis=axis, t...]
    all_to_all x1 -> x4, starting transfers between devices: 5.92 us -> 28.6 us  [swap(): lax.all_to_all(blocks, ('hi', 'lo'), split_axis=axis, concat_axis=axis, t...]
    pallas_call x3 -> x5, Pallas kernels: 72.2 us -> 89.5 us  [the longest x4 78.2 us: call(): pl.pallas_call(kernel, out_shape=[jax.ShapeDtypeStruct(one, jnp.float32)...]
  transfers between devices with their start and end apart: 1 -> 4, of which waited for: 1 -> 4; matrix products, arithmetic and copies ran while one was open for 0% -> 0% of each run, Pallas kernels for 0% -> 8%
where the time goes in v4:
time: 634 us; the launch traced here: 629 us
  waiting for transfers between devices  399 us (63%)
  blocking collectives  100 us (16%)
  Pallas kernels  99.3 us (16%)
  starting transfers between devices  28.6 us (5%)
    all_to_all x4, waiting for transfers between devices, swap(): lax.all_to_all(blocks, ('hi', 'lo'), split_axis=axis, concat_axis=axis, t...  399 us
    all_to_all x1, blocking collectives, swap(): lax.all_to_all(blocks, ('hi', 'lo'), split_axis=axis, concat_axis=axis, t...  100 us
    pallas_call x4, Pallas kernels, call(): pl.pallas_call(kernel, out_shape=[jax.ShapeDtypeStruct(one, jnp.float32)...  78.2 us
    all_to_all x4, starting transfers between devices, swap(): lax.all_to_all(blocks, ('hi', 'lo'), split_axis=axis, concat_axis=axis, t...  28.6 us
  transfers between devices with their start and end apart: 4, of which 4 were waited for; matrix products, arithmetic and copies ran while one was open for 0% of the time, Pallas kernels for 8%

profile of v4, /device:TPU:24, one launch (start us, length us, event | category | flops | bytes accessed | tf_op | source)
XLA Modules:
  0.0 629.5 jit_solution(9795468769409220386)
XLA Ops:
  0.0 9.8 %shard_map.91 = f32[64,256,128]{2,1,0:T(8,128)} custom-call(f32[16384,128]{1,0:T(8,128)} %bitcast.24), custom_call_target="tpu_custom_call" | custom-call | tf_op jit(solution)/shard_map/pallas_call | solution.py:180
  9.9 5.9 all-to-all-start
  15.8 0.1 fusion.13
  15.9 0.6 pad_maximum_fusion.1.rest_ref
  16.5 1.2 fusion.4
  17.7 0.8 pad_maximum_fusion
  18.5 178.7 %all-to-all-done = f32[32,512,128]{2,1,0:T(8,128)} async-done(((f32[32,512,128]{2,1,0:T(8,128)}), f32[32,512,128]{2,1,0:T(8,128)}, u32[]{:S(2)}, u32[]{:S(2)}) %all-to-all-start) | async-done | bytes 8388640 | tf_op jit(solution)/shard_map/all_to_all | solution.py:42
  197.2 26.4 %shard_map.92 = (f32[16384,128]{1,0:T(8,128)}, f32[8192,128]{1,0:T(8,128)}) custom-call(f32[16384,128]{1,0:T(8,128)} %bitcast.4.x_ref, bf16[64,192]{1,0:T(8,128)(2,1)} %constant.63.clone.t1_ref.t3_ref, bf16[256,1536]{1,0:T(8,128)(2,1)} %constant.64.clone.t2_ref, f32[2,32,32,8]{3,2,1,0:T(8,128)} %constant.69.own_ref, ...), custom_call_target="tpu_custom_call" | custom-call | flops 8000000000 | bytes 16777216 | tf_op jit(solution)/shard_map/pallas_call | solution.py:64
  223.6 6.8 %all-to-all-start.1 = ((f32[32,256,128]{2,1,0:T(8,128)}), f32[32,256,128]{2,1,0:T(8,128)}, u32[]{:S(2)}, u32[]{:S(2)}) async-start(f32[32,256,128]{2,1,0:T(8,128)} %bitcast.25), calls=%async_computation.1 | async-start | bytes 8388608 | tf_op jit(solution)/shard_map/all_to_all | solution.py:42
  230.4 10.6 %shard_map.94 = f32[8192,128]{1,0:T(8,128)} custom-call(f32[16384,128]{1,0:T(8,128)} %get-tuple-element.8.y_ref, bf16[256,1536]{1,0:T(8,128)(2,1)} %constant.65.clone.t2_ref, f32[2,128,128]{2,1,0:T(8,128)} %bitcast.29), custom_call_target="tpu_custom_call" | custom-call | flops 8000000000 | bytes 16777216 | tf_op jit(solution)/shard_map/pallas_call | solution.py:64
  241.0 80.0 %all-to-all-done.1 = f32[32,256,128]{2,1,0:T(8,128)} async-done(((f32[32,256,128]{2,1,0:T(8,128)}), f32[32,256,128]{2,1,0:T(8,128)}, u32[]{:S(2)}, u32[]{:S(2)}) %all-to-all-start.1) | async-done | bytes 4194336 | tf_op jit(solution)/shard_map/all_to_all | solution.py:42
  321.1 7.9 %all-to-all-start.3 = ((f32[32,256,128]{2,1,0:T(8,128)}), f32[32,256,128]{2,1,0:T(8,128)}, u32[]{:S(2)}, u32[]{:S(2)}) async-start(f32[32,256,128]{2,1,0:T(8,128)} %bitcast.27), calls=%async_computation.3 | async-start | bytes 8388608 | tf_op jit(solution)/shard_map/all_to_all | solution.py:42
  329.0 20.6 %shard_map.93 = f32[8192,128]{1,0:T(8,128)} custom-call(f32[8192,128]{1,0:T(8,128)} %bitcast.7.x_ref, bf16[64,192]{1,0:T(8,128)(2,1)} %constant.63.clone.t1_ref.t3_ref, bf16[256,768]{1,0:T(8,128)(2,1)} %constant.67.clone.t4_ref, f32[2,32,128]{2,1,0:T(8,128)} %constant.66.clone.turn_ref), custom_call_target="tpu_custom_call" | custom-call | flops 8000000000 | bytes 16777216 | tf_op jit(solution)/shard_map/pallas_call | solution.py:64
  349.6 70.0 %all-to-all-done.3 = f32[32,256,128]{2,1,0:T(8,128)} async-done(((f32[32,256,128]{2,1,0:T(8,128)}), f32[32,256,128]{2,1,0:T(8,128)}, u32[]{:S(2)}, u32[]{:S(2)}) %all-to-all-start.3) | async-done | bytes 4194336 | tf_op jit(solution)/shard_map/all_to_all | solution.py:42
  419.6 7.9 %all-to-all-start.2 = ((f32[32,256,128]{2,1,0:T(8,128)}), f32[32,256,128]{2,1,0:T(8,128)}, u32[]{:S(2)}, u32[]{:S(2)}) async-start(f32[32,256,128]{2,1,0:T(8,128)} %bitcast.26), calls=%async_computation.2 | async-start | bytes 8388608 | tf_op jit(solution)/shard_map/all_to_all | solution.py:42
  427.6 20.6 %shard_map.95 = f32[8192,128]{1,0:T(8,128)} custom-call(f32[8192,128]{1,0:T(8,128)} %bitcast.12.x_ref, bf16[64,192]{1,0:T(8,128)(2,1)} %constant.63.clone.t1_ref.t3_ref, bf16[256,768]{1,0:T(8,128)(2,1)} %constant.67.clone.t4_ref, f32[2,32,128]{2,1,0:T(8,128)} %constant.66.clone.turn_ref), custom_call_target="tpu_custom_call" | custom-call | flops 8000000000 | bytes 16777216 | tf_op jit(solution)/shard_map/pallas_call | solution.py:64
  448.2 70.0 %all-to-all-done.2 = f32[32,256,128]{2,1,0:T(8,128)} async-done(((f32[32,256,128]{2,1,0:T(8,128)}), f32[32,256,128]{2,1,0:T(8,128)}, u32[]{:S(2)}, u32[]{:S(2)}) %all-to-all-start.2) | async-done | bytes 4194336 | tf_op jit(solution)/shard_map/all_to_all | solution.py:42
  518.2 100.0 %all_to_all.25 = f32[32,256,128]{2,1,0:T(8,128)} all-to-all(f32[32,256,128]{2,1,0:T(8,128)} %bitcast.28), channel_id=1, replica_groups=mesh['hi'=4,'lo'=8] {'hi','lo'}, dimensions={0} | all-to-all | bytes 8388608 | tf_op jit(solution)/shard_map/all_to_all | solution.py:42
  618.2 11.2 %shard_map.96 = f32[16384,128]{1,0:T(8,128)} custom-call(f32[64,128,128]{2,1,0:T(8,128)} %bitcast.9.x0_ref, f32[64,128,128]{2,1,0:T(8,128)} %bitcast.23), custom_call_target="tpu_custom_call" | custom-call | tf_op jit(solution)/shard_map/pallas_call | solution.py:209
  (2 shorter events, 0.0 us)
Async XLA Ops:
  9.9 187.3 %all-to-all-start = ((f32[32,512,128]{2,1,0:T(8,128)}), f32[32,512,128]{2,1,0:T(8,128)}, u32[]{:S(2)}, u32[]{:S(2)}) async-start(f32[32,512,128]{2,1,0:T(8,128)} %bitcast.22), calls=%async_computation | async-start | bytes 16777216 | tf_op jit(solution)/shard_map/all_to_all | solution.py:42
  223.6 97.4 %all-to-all-start.1 = ((f32[32,256,128]{2,1,0:T(8,128)}), f32[32,256,128]{2,1,0:T(8,128)}, u32[]{:S(2)}, u32[]{:S(2)}) async-start(f32[32,256,128]{2,1,0:T(8,128)} %bitcast.25), calls=%async_computation.1 | async-start | bytes 8388608 | tf_op jit(solution)/shard_map/all_to_all | solution.py:42
  321.1 98.6 %all-to-all-start.3 = ((f32[32,256,128]{2,1,0:T(8,128)}), f32[32,256,128]{2,1,0:T(8,128)}, u32[]{:S(2)}, u32[]{:S(2)}) async-start(f32[32,256,128]{2,1,0:T(8,128)} %bitcast.27), calls=%async_computation.3 | async-start | bytes 8388608 | tf_op jit(solution)/shard_map/all_to_all | solution.py:42
  419.6 98.6 %all-to-all-start.2 = ((f32[32,256,128]{2,1,0:T(8,128)}), f32[32,256,128]{2,1,0:T(8,128)}, u32[]{:S(2)}, u32[]{:S(2)}) async-start(f32[32,256,128]{2,1,0:T(8,128)} %bitcast.26), calls=%async_computation.2 | async-start | bytes 8388608 | tf_op jit(solution)/shard_map/all_to_all | solution.py:42
